TPU v7x, 32 devices: a whole 2x2x4 slice. The times are simulated.
32 devices in a mesh: row: 2 (over y), col: 4 (over z), depth: 4 (over x, core).
Axes of the slice: x: 2, y: 2, z: 4, core: 2. Of those that a mesh axis runs over, the one named last changes fastest.
Arguments:
- grad_out: bfloat16 [1024, 6144], P('depth', 'col'), may hold values from -6 to 6
- pre_act: bfloat16 [1024, 24576], P('depth', 'row'), may hold values from -8 to 8
- down_weight: bfloat16 [24576, 6144], P(('row', 'depth'), 'col'), may hold values from -0.0546875 to 0.0546875
Outputs:
- grad_pre: bfloat16 [1024, 24576], P('depth', 'row')
- grad_weight: bfloat16 [24576, 6144], P(('row', 'depth'), 'col')
All inputs are finite; a program needn't handle non-finite values.
Results may differ from a plain program's by a relative error of at most 0.0066.
Values may be sent and summed in bfloat16 or wider, within the bound.
A program may use at most 128 MiB of HBM per device.

v0:
```python
import jax
import jax.numpy as jnp
from jax import lax
from jax.sharding import PartitionSpec as P

sqrt_two_pi = 0.7978845608028654
cubic_coeff = 0.044715


def gelu_value(preact):
    tangent = jnp.tanh(sqrt_two_pi * (preact + cubic_coeff * preact * preact * preact))
    return 0.5 * preact * (1.0 + tangent)


def gelu_slope(preact):
    tangent = jnp.tanh(sqrt_two_pi * (preact + cubic_coeff * preact * preact * preact))
    inner = sqrt_two_pi * (1.0 + 3.0 * cubic_coeff * preact * preact)
    return 0.5 * (1.0 + tangent) + 0.5 * preact * (1.0 - tangent * tangent) * inner


def contract_last(left, right):
    return lax.dot_general(
        left, right, (((1,), (1,)), ((), ())), preferred_element_type=jnp.float32
    )


def contract_first(left, right):
    return lax.dot_general(
        left, right, (((0,), (0,)), ((), ())), preferred_element_type=jnp.float32
    )


def finish_rows(partial_value, preacts):
    total = lax.psum(partial_value, "col")
    return (total * gelu_slope(preacts.astype(jnp.float32))).astype(jnp.bfloat16)


def on_device(grad_out, pre_act, down_weight):
    every_grad = lax.all_gather(grad_out, "depth", axis=0, tiled=True)
    own_pre = lax.all_to_all(pre_act, "depth", split_axis=1, concat_axis=0, tiled=True)
    partial_value = contract_last(every_grad, down_weight)
    local_grad = finish_rows(partial_value, own_pre)
    grad_pre = lax.all_to_all(local_grad, "depth", split_axis=0, concat_axis=1, tiled=True)
    own_act = gelu_value(own_pre.astype(jnp.float32)).astype(jnp.bfloat16)
    grad_weight = contract_first(own_act, every_grad).astype(jnp.bfloat16)
    return (grad_pre, grad_weight)


def solution(mesh):
    placed = (P("depth", "col"), P("depth", "row"), P(("row", "depth"), "col"))
    return jax.shard_map(
        on_device,
        mesh=mesh,
        in_specs=placed,
        out_specs=(P("depth", "row"), P(("row", "depth"), "col")),
        check_vma=False,
    )
```

profile of v0, /device:TPU:0, one launch (start us, length us, event | category | flops | bytes accessed | tf_op | source)
XLA Modules:
  0.0 588.5 jit_solution(14912220487641829081)
XLA Ops:
  7.2 0.0 all-gather.2.cloned.1.call-start
  7.2 0.7 all-gather.2.cloned.1.call-update
  7.9 0.0 all-reduce.2.cloned.1.call-start
  7.9 32.8 %all-gather.2.cloned.1.call-done = bf16[1024,1536]{1,0:T(8,128)(2,1)} async-done(((bf16[256,1536]{1,0:T(8,128)(2,1)}), bf16[1024,1536]{1,0:T(8,128)(2,1)}) %all-gather.2.cloned.1.call-update) | async-done | bytes 3145744 | tf_op jit(solution)/shard_map/all_gather | solution.py:39
  40.8 16.2 %fusion.11 = f32[1024,3072]{1,0:T(8,128)} fusion(bf16[1024,1536]{1,0:T(8,128)(2,1)} %all-gather.2.cloned.1.call-done, bf16[3072,1536]{1,0:T(8,128)(2,1)} %param.5), kind=kOutput, calls=%fused_computation.16 | convolution fusion | flops 9663676416 | bytes 25165824 | tf_op jit(solution)/shard_map/dot_general | solution.py:22
  57.0 0.0 all-reduce.2.cloned.1.call-update
  57.0 3.2 copy.10
  60.2 74.3 %all_to_all.32 = bf16[256,4,3072]{2,0,1:T(8,128)(2,1)} all-to-all(bf16[256,4,3072]{2,0,1:T(8,128)(2,1)S(1)} %bitcast.30), channel_id=1, replica_groups=mesh['row'=2,'col'=4,'depth'=4] {'depth'}, dimensions={1} | all-to-all | bytes 12582912 | tf_op jit(solution)/shard_map/all_to_all | solution.py:40
  134.5 348.8 %all-reduce.2.cloned.1.call-done = f32[1024,3072]{1,0:T(8,128)} async-done(((f32[1024,3072]{1,0:T(8,128)}), f32[1024,3072]{1,0:T(8,128)}) %all-reduce.2.cloned.1.call-update) | async-done | bytes 12582928 | tf_op jit(solution)/shard_map/psum | solution.py:34
  483.3 16.1 %fusion.10 = (bf16[1024,3072]{1,0:T(8,128)(2,1)}, bf16[1024,3072]{1,0:T(8,128)(2,1)}) fusion(bf16[256,4,3072]{2,0,1:T(8,128)(2,1)} %all_to_all.32, f32[1024,3072]{1,0:T(8,128)} %all-reduce.2.cloned.1.call-done), kind=kLoop, calls=%fused_computation.13 | loop fusion | flops 69206016 | bytes 31457280 | tf_op jit(solution)/shard_map/convert_element_type | solution.py:44
  499.4 0.0 copy-start
  499.4 5.5 all-to-all-start.1
  504.9 0.0 copy-done
  504.9 14.9 %convolution_convert_fusion = bf16[3072,1536]{1,0:T(8,128)(2,1)} fusion(bf16[1024,3072]{1,0:T(8,128)(2,1)} %get-tuple-element.2, bf16[1024,1536]{1,0:T(8,128)(2,1)S(1)} %copy-done), kind=kOutput, calls=%fused_computation.14 | convolution fusion | flops 9668395008 | bytes 18874368 | tf_op jit(solution)/shard_map/dot_general | solution.py:28
  519.8 55.7 %all-to-all-done.1 = bf16[4,256,3072]{2,1,0:T(8,128)(2,1)} async-done(((bf16[4,256,3072]{2,1,0:T(8,128)(2,1)}), bf16[4,256,3072]{2,1,0:T(8,128)(2,1)}, u32[]{:S(2)}, u32[]{:S(2)}) %all-to-all-start.1) | async-done | bytes 6291488 | tf_op jit(solution)/shard_map/all_to_all | solution.py:43
  575.6 6.1 %copy.8 = bf16[4,32,8,3072]{3,2,0,1:T(8,128)(2,1)} copy(bf16[4,32,8,3072]{3,2,1,0:T(8,128)(2,1)} %bitcast.7) | data formatting | bytes 12582912 | tf_op jit(solution)/shard_map/all_to_all | solution.py:43
Async XLA Ops:
  7.2 33.6 %all-gather.2.cloned.1.call-start = ((), (), s32[]{:S(2)}) async-start(), calls=%async_computation.2 | async-start | bytes 3932160 | tf_op jit(solution)/shard_map/all_gather | solution.py:39
  7.9 475.4 %all-reduce.2.cloned.1.call-start = ((), (), s32[]{:S(2)}) async-start(), calls=%async_computation.3 | async-start | bytes 25165824 | tf_op jit(solution)/shard_map/psum | solution.py:34
  499.4 5.5 copy-start
  499.4 76.2 %all-to-all-start.1 = ((bf16[4,256,3072]{2,1,0:T(8,128)(2,1)}), bf16[4,256,3072]{2,1,0:T(8,128)(2,1)}, u32[]{:S(2)}, u32[]{:S(2)}) async-start(bf16[4,256,3072]{2,1,0:T(8,128)(2,1)} %bitcast.31), calls=%async_computation.1 | async-start | bytes 12582912 | tf_op jit(solution)/shard_map/all_to_all | solution.py:43
Sparse Core Ops, SparseCore 0:
  9.5 31.2 all-gather.1
  57.1 426.1 all-reduce.1
where the time goes:
time: 589 us
  waiting for transfers between devices  438 us (74%)
  blocking collectives  74.3 us (13%)
  matrix products  31.1 us (5%)
  other arithmetic  16.1 us (3%)
  between operations  14.1 us (2%)
  local copies, waits for them, and re-layouts  9.36 us (2%)
    psum x1, waiting for transfers between devices, finish_rows(): total = lax.psum(partial_value, 'col')  349 us
    all_to_all x1, blocking collectives, on_device(): lax.all_to_all(pre_act, 'depth', split_axis=1, concat_axis=0, tiled=True)  74.3 us
    all_to_all x1, waiting for transfers between devices, on_device(): lax.all_to_all(local_grad, 'depth', split_axis=0, concat_axis=1, tiled=True)  55.7 us
    all_gather x1, waiting for transfers between devices, on_device(): every_grad = lax.all_gather(grad_out, 'depth', axis=0, tiled=True)  32.8 us
    dot_general x1, matrix products, contract_last(): lax.dot_general(left, right, (((1,), (1,)), ((), ())), preferred_element_...  16.2 us
    convert_element_type x1, other arithmetic, on_device(): own_act = gelu_value(own_pre.astype(jnp.float32)).astype(jnp.bfloat16)  16.1 us
    dot_general x1, matrix products, contract_first(): lax.dot_general(left, right, (((0,), (0,)), ((), ())), preferred_element_...  14.9 us
  transfers between devices with their start and end apart: 3, of which 3 were waited for; matrix products, arithmetic and copies ran while one was open for 3% of the time, Pallas kernels for 0%

commit v1 on v0

--- a/solution.py
+++ b/solution.py
@@ -1,3 +1,4 @@
+import functools
 import jax
 import jax.numpy as jnp
 from jax import lax
@@ -5,6 +6,26 @@
 
 sqrt_two_pi = 0.7978845608028654
 cubic_coeff = 0.044715
+
+
+def open_figure_on_mesh(local_block, bus_axis):
+    n_shards = lax.axis_size(bus_axis)
+
+    def expand_sheets(y2, h_now):
+        if h_now >= n_shards:
+            return y2
+        so_far_all = []
+        for i in range(n_shards):
+            so_far_all.append((i, i ^ h_now))
+        shaped = lax.ppermute(y2, bus_axis, so_far_all)
+        k_now = expand_sheets(y2 + shaped, 2 * h_now)
+        return k_now
+
+    formed = expand_sheets(local_block, 1)
+    return formed
+
+
+_draft_ways = functools.partial(open_figure_on_mesh, bus_axis="col")
 
 
 def gelu_value(preact):
@@ -31,7 +52,7 @@
 
 
 def finish_rows(partial_value, preacts):
-    total = lax.psum(partial_value, "col")
+    total = _draft_ways(partial_value)
     return (total * gelu_slope(preacts.astype(jnp.float32))).astype(jnp.bfloat16)
 
 

time: 589 us -> 984 us (1.67)
  waiting for transfers between devices: 438 us -> 820 us
    ppermute x0 -> x2, waiting for transfers between devices: none -> 731 us  [expand_sheets(): shaped = lax.ppermute(y2, bus_axis, so_far_all)]
    psum x1 -> x0, waiting for transfers between devices: 349 us -> none  [finish_rows(): total = lax.psum(partial_value, 'col')]
  transfers between devices with their start and end apart: 3 -> 4, of which waited for: 3 -> 4; matrix products, arithmetic and copies ran while one was open for 3% -> 2% of each run, Pallas kernels for 0% -> 0%
where the time goes in v1:
time: 984 us
  waiting for transfers between devices  820 us (83%)
  blocking collectives  74.2 us (8%)
  matrix products  28.4 us (3%)
  other arithmetic  25.5 us (3%)
  between operations  14.1 us (1%)
  local copies, waits for them, and re-layouts  12.3 us (1%)
    ppermute x2, waiting for transfers between devices, expand_sheets(): shaped = lax.ppermute(y2, bus_axis, so_far_all)  731 us
    all_to_all x1, blocking collectives, on_device(): lax.all_to_all(pre_act, 'depth', split_axis=1, concat_axis=0, tiled=True)  74.2 us
    all_to_all x1, waiting for transfers between devices, on_device(): lax.all_to_all(local_grad, 'depth', split_axis=0, concat_axis=1, tiled=True)  55.6 us
    all_gather x1, waiting for transfers between devices, on_device(): every_grad = lax.all_gather(grad_out, 'depth', axis=0, tiled=True)  32.9 us
  transfers between devices with their start and end apart: 4, of which 4 were waited for; matrix products, arithmetic and copies ran while one was open for 2% of the time, Pallas kernels for 0%

profile of v1, /device:TPU:0, one launch (start us, length us, event | category | flops | bytes accessed | tf_op | source)
XLA Modules:
  0.0 983.9 jit_solution(17481418890469063984)
XLA Ops:
  7.2 0.0 all-gather.2.cloned.1.call-start
  7.2 0.7 all-gather.2.cloned.1.call-update
  7.9 32.9 %all-gather.2.cloned.1.call-done = bf16[1024,1536]{1,0:T(8,128)(2,1)} async-done(((bf16[256,1536]{1,0:T(8,128)(2,1)}), bf16[1024,1536]{1,0:T(8,128)(2,1)}) %all-gather.2.cloned.1.call-update) | async-done | bytes 3145744 | tf_op jit(solution)/shard_map/all_gather | solution.py:60
  40.8 13.5 %fusion.11 = f32[1024,3072]{1,0:T(8,128)S(1)} fusion(bf16[1024,1536]{1,0:T(8,128)(2,1)} %all-gather.2.cloned.1.call-done, bf16[3072,1536]{1,0:T(8,128)(2,1)} %param.5), kind=kOutput, calls=%fused_computation.16 | convolution fusion | flops 9663676416 | bytes 25165824 | tf_op jit(solution)/shard_map/dot_general | solution.py:43
  54.3 0.0 copy-start
  54.3 1.6 collective-permute-start
  55.8 3.0 copy-done
  58.8 268.1 %collective-permute-done = f32[1024,3072]{1,0:T(8,128)} collective-permute-done((f32[1024,3072]{1,0:T(8,128)S(1)}, f32[1024,3072]{1,0:T(8,128)}, u32[]{:S(2)}, u32[]{:S(2)}) %collective-permute-start) | collective-permute-done | bytes 12582944 | tf_op jit(solution)/shard_map/ppermute | solution.py:20
  326.9 9.5 add.20
  336.4 2.5 collective-permute-start.1
  338.9 3.2 copy.10
  342.1 74.2 %all_to_all.32 = bf16[256,4,3072]{2,0,1:T(8,128)(2,1)} all-to-all(bf16[256,4,3072]{2,0,1:T(8,128)(2,1)S(1)} %bitcast.30), channel_id=1, replica_groups=mesh['row'=2,'col'=4,'depth'=4] {'depth'}, dimensions={1} | all-to-all | bytes 12582912 | tf_op jit(solution)/shard_map/all_to_all | solution.py:61
  416.3 462.4 %collective-permute-done.1 = f32[1024,3072]{1,0:T(8,128)} collective-permute-done((f32[1024,3072]{1,0:T(8,128)S(1)}, f32[1024,3072]{1,0:T(8,128)}, u32[]{:S(2)}, u32[]{:S(2)}) %collective-permute-start.1) | collective-permute-done | bytes 12582944 | tf_op jit(solution)/shard_map/ppermute | solution.py:20
  878.7 16.1 %fusion.10 = (bf16[1024,3072]{1,0:T(8,128)(2,1)}, bf16[1024,3072]{1,0:T(8,128)(2,1)}) fusion(bf16[256,4,3072]{2,0,1:T(8,128)(2,1)} %all_to_all.32, f32[1024,3072]{1,0:T(8,128)S(1)} %add.20, f32[1024,3072]{1,0:T(8,128)} %collective-permute-done.1), kind=kLoop, calls=%fused_computation.13 | loop fusion | flops 72351744 | bytes 44040192 | tf_op jit(solution)/shard_map/convert_element_type | solution.py:65
  894.8 0.0 copy-start.1
  894.8 5.7 all-to-all-start.1
  900.5 0.0 copy-done.1
  900.5 14.9 %convolution_convert_fusion = bf16[3072,1536]{1,0:T(8,128)(2,1)} fusion(bf16[1024,3072]{1,0:T(8,128)(2,1)} %get-tuple-element.2, bf16[1024,1536]{1,0:T(8,128)(2,1)S(1)} %copy-done.1), kind=kOutput, calls=%fused_computation.14 | convolution fusion | flops 9668395008 | bytes 18874368 | tf_op jit(solution)/shard_map/dot_general | solution.py:49
  915.4 55.6 %all-to-all-done.1 = bf16[4,256,3072]{2,1,0:T(8,128)(2,1)} async-done(((bf16[4,256,3072]{2,1,0:T(8,128)(2,1)}), bf16[4,256,3072]{2,1,0:T(8,128)(2,1)}, u32[]{:S(2)}, u32[]{:S(2)}) %all-to-all-start.1) | async-done | bytes 6291488 | tf_op jit(solution)/shard_map/all_to_all | solution.py:64
  971.0 6.1 copy.8
Async XLA Ops:
  7.2 33.6 %all-gather.2.cloned.1.call-start = ((), (), s32[]{:S(2)}) async-start(), calls=%async_computation.2 | async-start | bytes 3932160 | tf_op jit(solution)/shard_map/all_gather | solution.py:60
  54.3 4.5 copy-start
  54.3 272.6 %collective-permute-start = (f32[1024,3072]{1,0:T(8,128)S(1)}, f32[1024,3072]{1,0:T(8,128)}, u32[]{:S(2)}, u32[]{:S(2)}) collective-permute-start(f32[1024,3072]{1,0:T(8,128)S(1)} %fusion.11), channel_id=1, source_target_pairs={{0,4},{4,0},{8,12},{12,8},{1,5},{5,1},{9,13},{13,9},{2,6},{6,2},{1... | collective-permute-start | bytes 37748744 | tf_op jit(solution)/shard_map/ppermute | solution.py:20
  336.4 542.3 %collective-permute-start.1 = (f32[1024,3072]{1,0:T(8,128)S(1)}, f32[1024,3072]{1,0:T(8,128)}, u32[]{:S(2)}, u32[]{:S(2)}) collective-permute-start(f32[1024,3072]{1,0:T(8,128)S(1)} %add.20), channel_id=1, source_target_pairs={{0,8},{4,12},{8,0},{12,4},{1,9},{5,13},{9,1},{13,5},{2,10},{6,14},... | collective-permute-start | bytes 37748744 | tf_op jit(solution)/shard_map/ppermute | solution.py:20
  894.8 5.7 copy-start.1
  894.8 76.2 %all-to-all-start.1 = ((bf16[4,256,3072]{2,1,0:T(8,128)(2,1)}), bf16[4,256,3072]{2,1,0:T(8,128)(2,1)}, u32[]{:S(2)}, u32[]{:S(2)}) async-start(bf16[4,256,3072]{2,1,0:T(8,128)(2,1)} %bitcast.31), calls=%async_computation.1 | async-start | bytes 12582912 | tf_op jit(solution)/shard_map/all_to_all | solution.py:64
Sparse Core Ops, SparseCore 0:
  9.5 31.2 all-gather.1
